TPU v7x, 32 devices: a whole 2x2x4 slice. The times are simulated.
32 devices in a mesh: snap: 4 (over x, core), lag: 8 (over z, y).
Axes of the slice: x: 2, y: 2, z: 4, core: 2. Of those that a mesh axis runs over, the one named last changes fastest.
Arguments:
- snapshots: bfloat16 [2, 16384, 256], P(None, 'snap', 'lag')
- positions: int32 [256], replicated, may hold values from 0 to 16383, as said below
- counts: int32 [4], P('snap'), may hold values from 1 to 4096, 8192 in all
- initial: float32 [2, 96, 16384], P(None, None, 'lag'), may hold values from -6 to 6
Outputs:
- lag_corr: float32 [2, 16384], P(None, 'lag')
- subspace: float32 [2, 96, 16384], P(None, None, 'lag')
Inputs may be any that keep to these rules, and one draw needn't show every extreme that they name: `positions`: positions are distinct; 0 and 16383 are among them.
All inputs are finite; a program needn't handle non-finite values. No bound on the sum of `counts` on one device may be relied on, other than what follows from the above.
Results may differ from a plain program's by a relative error of at most 0.0003.
Values may be sent and summed in bfloat16 or wider, within the bound.
No kernel may reach another device: no remote copies, remote signals or barrier semaphores. Data moves between devices by JAX's collectives and lax.ppermute only.
A program may use at most 64 MiB of HBM per device.

v0:
```python
import math
import jax
import jax.numpy as jnp
from jax import lax
from jax.sharding import PartitionSpec as P

ITERS = 2
exact = lax.Precision.HIGHEST


def correlate(former, latter):

    def product(left_rows, right_rows):
        return jnp.einsum("ta,tb->ab", left_rows, right_rows, preferred_element_type=jnp.float32)

    real_part = product(former[0], latter[0]) + product(former[1], latter[1])
    imag_part = product(former[1], latter[0]) - product(former[0], latter[1])
    return jnp.stack([real_part, imag_part])


def bin_pairs(values, pair_lags, width):
    low_count = math.gcd(width, 128)
    high_count = width // low_count
    pair_total = pair_lags.shape[0]
    block_size = math.gcd(pair_total, 1024)
    low_ids = jnp.arange(low_count, dtype=jnp.int32)
    high_ids = jnp.arange(high_count, dtype=jnp.int32)

    def accumulate(turn_index, running):
        segment_lags = lax.dynamic_slice_in_dim(pair_lags, turn_index * block_size, block_size)
        segment_values = lax.dynamic_slice_in_dim(values, turn_index * block_size, block_size, 0)
        inside = (segment_lags >= 0) & (segment_lags < width)
        high_hot = (
            ((segment_lags // low_count)[:, None] == high_ids[None, :]) & inside[:, None]
        ).astype(jnp.float32)
        low_hot = ((segment_lags % low_count)[:, None] == low_ids[None, :]).astype(jnp.float32)
        weighted = segment_values[:, :, None] * low_hot[:, None, :]
        return running + jnp.einsum("ph,pcl->chl", high_hot, weighted, precision=exact)

    empty = jnp.zeros((values.shape[1], high_count, low_count), jnp.float32)
    running = lax.fori_loop(0, pair_total // block_size, accumulate, empty)
    return running.reshape(values.shape[1], width)


def rotation(row_ids, col_ids, period, direction):
    turns = row_ids[:, None] * col_ids[None, :] % period
    angle = direction * 2.0 * math.pi / period * turns.astype(jnp.float32)
    return (jnp.cos(angle), jnp.sin(angle))


def rotate(table, values, form):
    cosine, sine = table
    real_part = jnp.einsum(form, cosine, values[0], precision=exact) - jnp.einsum(
        form, sine, values[1], precision=exact
    )
    imag_part = jnp.einsum(form, sine, values[0], precision=exact) + jnp.einsum(
        form, cosine, values[1], precision=exact
    )
    return jnp.stack([real_part, imag_part])


def twist(table, values):
    cosine, sine = table
    return jnp.stack([cosine * values[0] - sine * values[1], sine * values[0] + cosine * values[1]])


def split_length(length):
    padded = 2 * length
    first = math.gcd(padded, 2 ** (padded.bit_length() // 2))
    return (padded, first, padded // first)


def local_forward(values):
    length = values.shape[2]
    padded, first, second = split_length(length)
    half = first // 2
    shaped = values.reshape(2, values.shape[1], half, second)
    first_ids = jnp.arange(first, dtype=jnp.int32)
    half_ids = jnp.arange(half, dtype=jnp.int32)
    second_ids = jnp.arange(second, dtype=jnp.int32)
    sectioned = rotate(rotation(first_ids, half_ids, first, -1.0), shaped, "kt,ats->aks")
    sectioned = twist(rotation(first_ids, second_ids, padded, -1.0), sectioned)
    return rotate(rotation(second_ids, second_ids, second, -1.0), sectioned, "sq,aks->akq")


def local_inverse(spectra, length):
    padded, first, second = split_length(length)
    half = first // 2
    first_ids = jnp.arange(first, dtype=jnp.int32)
    half_ids = jnp.arange(half, dtype=jnp.int32)
    second_ids = jnp.arange(second, dtype=jnp.int32)
    sectioned = rotate(rotation(second_ids, second_ids, second, 1.0), spectra, "qs,akq->aks")
    sectioned = twist(rotation(first_ids, second_ids, padded, 1.0), sectioned)
    result = rotate(rotation(half_ids, first_ids, first, 1.0), sectioned, "tk,aks->ats") / padded
    return result.reshape(2, spectra.shape[1], length)


def transpose_apply(columns, spec_table):
    spread = lax.all_to_all(columns, "lag", split_axis=1, concat_axis=2, tiled=True)
    length = spread.shape[2]
    images = local_inverse(local_forward(spread) * spec_table[None, None], length)
    back = lax.all_to_all(images, "lag", split_axis=2, concat_axis=1, tiled=True)
    return back


def orthonormalize(mapped, identity, lag_total):
    partial_gram = jnp.einsum("xaj,xbj->ab", mapped, mapped, precision=exact)
    gram_matrix = lax.psum(partial_gram, "lag") / lag_total
    factor = jnp.linalg.cholesky(gram_matrix)
    inverse = lax.linalg.triangular_solve(factor, identity, left_side=True, lower=True)
    return jnp.einsum("ab,xbj->xaj", inverse, mapped, precision=exact)


def on_device(snapshots, positions, counts, initial):
    rows_here = snapshots.shape[1]
    sensors_here = snapshots.shape[2]
    lag_index = lax.axis_index("lag")
    lag_dev = initial.shape[2]
    lag_total = lag_dev * lax.axis_size("lag")
    live_rows = jnp.arange(rows_here, dtype=jnp.int32) < counts[0]
    masked = jnp.where(live_rows[None, :, None], snapshots, jnp.zeros((), snapshots.dtype))
    correlations = correlate(masked, lax.all_gather(masked, "lag", axis=2, tiled=True))
    own_positions = lax.dynamic_slice_in_dim(positions, lag_index * sensors_here, sensors_here)
    pair_lags = (own_positions[:, None] - positions[None, :]).reshape(-1)
    values = jnp.stack(
        [
            correlations[0].reshape(-1),
            correlations[1].reshape(-1),
            (pair_lags >= 0).astype(jnp.float32),
        ],
        1,
    )
    lag_sums = lax.psum_scatter(
        bin_pairs(values, pair_lags, lag_dev * lax.axis_size("lag")).T,
        "lag",
        scatter_dimension=0,
        tiled=True,
    ).T
    binned, snap_total = lax.psum((lag_sums[:2], jnp.sum(counts).astype(jnp.float32)), "snap")
    lag_corr = binned / (jnp.maximum(lag_sums[2], 1.0) * snap_total)
    global_ids = lag_index * lag_dev + jnp.arange(lag_dev, dtype=jnp.int32)
    halved = lag_corr * jnp.where(global_ids == 0, 0.5, 1.0)[None, :]
    column_count = initial.shape[1]
    columns = initial
    identity = jnp.eye(column_count, dtype=jnp.float32)
    whole_corr = lax.all_gather(halved, "lag", axis=1, tiled=True)
    spec_table = 2.0 * local_forward(whole_corr[:, None, :])[0, 0]
    for sweep in range(ITERS):
        mapped = transpose_apply(columns, spec_table)
        columns = orthonormalize(mapped, identity, lag_total)
    return (lag_corr, columns)


def solution(mesh):
    return jax.shard_map(
        on_device,
        mesh=mesh,
        in_specs=(P(None, "snap", "lag"), P(), P("snap"), P(None, None, "lag")),
        out_specs=(P(None, "lag"), P(None, None, "lag")),
        check_vma=False,
    )
```

profile of v0, /device:TPU:2, one launch (start us, length us, event | category | flops | bytes accessed | tf_op | source)
XLA Modules:
  0.0 859.2 jit_solution(15518628478419992472)
XLA Ops:
  12.3 6.0 all-to-all-start
  19.7 54.4 %all-to-all-done = f32[2,96,2048]{2,0,1:T(2,128)S(1)} async-done(((f32[2,96,2048]{2,0,1:T(2,128)}), f32[2,96,2048]{2,0,1:T(2,128)S(1)}, u32[]{:S(2)}, u32[]{:S(2)}) %all-to-all-start) | async-done | bytes 1572896 | tf_op jit(solution)/shard_map/all_to_all | solution.py:99
  90.3 17.6 %all-gather.2.cloned.1.call-done = bf16[2,4096,256]{1,2,0:T(8,128)(2,1)} async-done(((bf16[2,4096,32]{1,2,0:T(8,128)(2,1)}), bf16[2,4096,256]{1,2,0:T(8,128)(2,1)}) %all-gather.2.cloned.1.call-update) | async-done | bytes 4194320 | tf_op jit(solution)/shard_map/all_gather | solution.py:122
  114.4 24.5 %while.17 = (s32[]{:T(128)}, f32[3,128,128]{1,2,0:T(8,128)}, f32[8192,3]{0,1:T(4,128)S(1)}, s32[8192]{0:T(1024)S(1)}, s32[]{:T(128)}, /*index=5*/s32[]{:T(128)}, s32[]{:T(128)}, s32[]{:T(128)}) while((s32[]{:T(128)}, f32[3,128,128]{1,2,0:T(8,128)}, f32[8192,3]{0,1:T(4,128)S(1)}, s32[8192]{0:T(1024)S(1)}, s32[]{:T(128)}, ...), condition=%wide.region_1.2_spmd.clone.clone, body=%wide.region_0.1_spmd.clone.clone.sunk | while | flops 605024256 | bytes 2560165 | solution.py:41
  140.1 5.1 copy.139
  145.2 4.8 add_bitcast_fusion.1
  153.0 138.3 %reduce-scatter.4.cloned.1.call-done = f32[2048,3]{1,0:T(8,128)} async-done(((f32[16384,3]{1,0:T(8,128)}), f32[2048,3]{1,0:T(8,128)}) %reduce-scatter.4.cloned.1.call-update) | async-done | bytes 24592
  292.9 10.4 %all-reduce = (f32[2,2048]{1,0:T(2,128)S(1)}, f32[]{:T(128)}) all-reduce(f32[2,2048]{1,0:T(2,128)S(1)} %slice.94, f32[]{:T(128)S(6)} %convert_element_type.188), channel_id=1, replica_groups=mesh['snap'=4,'lag'=8] {'snap'}, use_global_device_ids=true, to_apply=%region_3.4 | all-reduce | flops 4097 | bytes 32776 | tf_op jit(solution)/shard_map/psum | solution.py:139
  304.6 30.7 %all_gather.7 = f32[2,16384]{1,0:T(2,128)S(1)} all-gather(f32[2,2048]{1,0:T(2,128)S(1)} %get-tuple-element.212), channel_id=1, replica_groups=mesh['snap'=4,'lag'=8] {'lag'}, dimensions={1}, use_global_device_ids=true | all-gather | bytes 147456 | tf_op jit(solution)/shard_map/all_gather | solution.py:146
  364.0 5.3 fusion.51
  373.3 15.2 %copy.83 = f32[2,12,16384]{1,0,2:T(2,128)} copy(f32[2,12,16384]{2,1,0:T(8,128)S(1)} %maximum_multiply_fusion.2) | data formatting | bytes 3145728 | tf_op jit(solution)/shard_map/div | solution.py:94
  388.4 28.6 %reshape.267 = f32[8,1,49152]{2,1,0:T(1,128)S(1)} reshape(f32[16384,2,12]{2,1,0:T(2,128)} %bitcast.290) | data formatting | bytes 3145728
  417.0 35.2 %all_to_all.66 = f32[8,1,49152]{2,1,0:T(1,128)S(1)} all-to-all(f32[8,1,49152]{2,1,0:T(1,128)S(1)} %reshape.267), channel_id=1, replica_groups=mesh['snap'=4,'lag'=8] {'lag'}, dimensions={0} | all-to-all | bytes 3145728 | tf_op jit(solution)/shard_map/all_to_all | solution.py:102
  452.7 4.4 reduce.4
  457.1 32.7 %reshape.268 = f32[16384,2,12]{2,1,0:T(2,128)} reshape(f32[8,49152]{1,0:T(8,128)S(1)} %reduce.4) | data formatting | bytes 3145728
  489.8 13.5 %copy.135 = f32[2,12,8,2048]{3,2,0,1:T(8,128)S(1)} copy(f32[2,12,8,2048]{1,0,3,2:T(2,128)} %bitcast.291) | data formatting | bytes 3145728 | tf_op jit(solution)/shard_map/all_to_all | solution.py:102
  507.6 36.0 %psum.30 = f32[96,96]{0,1:T(8,128)S(1)} all-reduce(f32[96,96]{0,1:T(8,128)S(1)} %fusion.55), channel_id=1, replica_groups=mesh['snap'=4,'lag'=8] {'lag'}, use_global_device_ids=true, to_apply=%region_5.6 | all-reduce | flops 9216 | bytes 73728 | tf_op jit(solution)/shard_map/psum | solution.py:108
  543.7 8.8 %cholesky.44 = f32[96,96]{1,0:T(8,128)S(1)} custom-call(f32[96,96]{1,0:T(8,128)S(1)} %fusion.186), custom_call_target="Cholesky" | custom-call | tf_op jit(solution)/shard_map/jit(cholesky)/cholesky | solution.py:109
  553.8 7.4 custom-call.7
  570.4 28.5 %all-to-all-done.2 = f32[2,96,2048]{2,0,1:T(2,128)S(1)} async-done(((f32[2,96,2048]{2,0,1:T(2,128)}), f32[2,96,2048]{2,0,1:T(2,128)S(1)}, u32[]{:S(2)}, u32[]{:S(2)}) %all-to-all-start.2) | async-done | bytes 1572896 | tf_op jit(solution)/shard_map/all_to_all | solution.py:99
  637.1 4.0 fusion.68
  641.0 4.1 fusion.48
  649.7 5.1 fusion.49
  658.8 15.2 %copy.109 = f32[2,12,16384]{1,0,2:T(2,128)} copy(f32[2,12,16384]{2,1,0:T(8,128)S(1)} %maximum_multiply_fusion.3) | data formatting | bytes 3145728 | tf_op jit(solution)/shard_map/div | solution.py:94
  674.0 28.6 %reshape.269 = f32[8,1,49152]{2,1,0:T(1,128)S(1)} reshape(f32[16384,2,12]{2,1,0:T(2,128)} %bitcast.292) | data formatting | bytes 3145728
  702.6 37.1 %all_to_all.67 = f32[8,1,49152]{2,1,0:T(1,128)S(1)} all-to-all(f32[8,1,49152]{2,1,0:T(1,128)S(1)} %reshape.269), channel_id=1, replica_groups=mesh['snap'=4,'lag'=8] {'lag'}, dimensions={0} | all-to-all | bytes 3145728 | tf_op jit(solution)/shard_map/all_to_all | solution.py:102
  739.7 4.4 reduce.5
  744.1 32.9 %reshape.270 = f32[16384,2,12]{2,1,0:T(2,128)} reshape(f32[8,49152]{1,0:T(8,128)S(1)} %reduce.5) | data formatting | bytes 3145728
  777.0 13.5 %copy.137 = f32[2,12,8,2048]{3,2,0,1:T(8,128)S(1)} copy(f32[2,12,8,2048]{1,0,3,2:T(2,128)} %bitcast.293) | data formatting | bytes 3145728 | tf_op jit(solution)/shard_map/all_to_all | solution.py:102
  794.8 36.0 %psum.31 = f32[96,96]{0,1:T(8,128)S(1)} all-reduce(f32[96,96]{0,1:T(8,128)S(1)} %fusion.58), channel_id=1, replica_groups=mesh['snap'=4,'lag'=8] {'lag'}, use_global_device_ids=true, to_apply=%region_8.11 | all-reduce | flops 9216 | bytes 73728 | tf_op jit(solution)/shard_map/psum | solution.py:108
  830.9 8.8 %cholesky.55 = f32[96,96]{1,0:T(8,128)S(1)} custom-call(f32[96,96]{1,0:T(8,128)S(1)} %fusion.184), custom_call_target="Cholesky" | custom-call | tf_op jit(solution)/shard_map/jit(cholesky)/cholesky | solution.py:109
  841.0 7.4 custom-call.8
  (198 shorter events, 163.5 us)
Async XLA Ops:
  7.2 2.8 copy-start.11
  7.2 100.7 %all-gather.2.cloned.1.call-start = ((), (), s32[]{:S(2)}) async-start(), calls=%async_computation.5 | async-start | bytes 4718592 | tf_op jit(solution)/shard_map/all_gather | solution.py:122
  12.3 6.0 copy-start.14
  12.3 61.9 %all-to-all-start = ((f32[2,96,2048]{2,0,1:T(2,128)}), f32[2,96,2048]{2,0,1:T(2,128)S(1)}, u32[]{:S(2)}, u32[]{:S(2)}) async-start(f32[2,96,2048]{2,0,1:T(2,128)} %copy.74), calls=%async_computation | async-start | bytes 3145728 | tf_op jit(solution)/shard_map/all_to_all | solution.py:99
  18.2 273.0 %reduce-scatter.4.cloned.1.call-start = ((), (), s32[]{:S(2)}) async-start(), calls=%async_computation.6 | async-start | bytes 9437184
  19.2 130.9 %copy-start.5 = (f32[256,128]{1,0:T(8,128)}, f32[256,128]{1,0:T(8,128)S(1)}, u32[]{:S(2)}) copy-start(f32[256,128]{1,0:T(8,128)S(1)} %get-tuple-element.220) | copy-start | bytes 393220
  84.1 2.9 copy-start
  87.0 20.9 %copy-start.10 = (bf16[2,4096,32]{1,2,0:T(8,128)(2,1)S(1)}, bf16[2,4096,32]{1,2,0:T(8,128)(2,1)}, u32[]{:S(2)}) copy-start(bf16[2,4096,32]{1,2,0:T(8,128)(2,1)} %broadcast_select_fusion) | copy-start | bytes 1572868
  107.9 4.9 copy-start.15
  145.2 4.9 copy-start.1
  145.2 4.9 copy-start.2
  336.1 4.5 copy-start.4
  336.9 3.7 copy-start.3
  340.7 0.7 copy-start.12
  369.3 2.6 copy-start.8
  566.3 3.9 copy-start.6
  566.3 32.6 %all-to-all-start.2 = ((f32[2,96,2048]{2,0,1:T(2,128)}), f32[2,96,2048]{2,0,1:T(2,128)S(1)}, u32[]{:S(2)}, u32[]{:S(2)}) async-start(f32[2,96,2048]{2,0,1:T(2,128)} %copy.91), calls=%async_computation.2 | async-start | bytes 3145728 | tf_op jit(solution)/shard_map/all_to_all | solution.py:99
  604.9 1.9 copy-start.9
  623.6 3.0 copy-start.13
  654.8 2.6 copy-start.7
Sparse Core Ops, SparseCore 0:
  10.2 97.6 all-gather.1
  145.3 145.9 reduce-scatter.3
where the time goes:
time: 871 us; the launch traced here: 859 us
  waiting for transfers between devices  239 us (27%)
  local copies, waits for them, and re-layouts  221 us (25%)
  blocking collectives  185 us (21%)
  matrix products  135 us (15%)
  other arithmetic  53.5 us (6%)
  between operations  15.8 us (2%)
  starting transfers between devices  9.92 us (1%)
    unnamed x3, waiting for transfers between devices  138 us
    unnamed x44, local copies, waits for them, and re-layouts  132 us
    all_to_all x2, waiting for transfers between devices, transpose_apply(): lax.all_to_all(columns, 'lag', split_axis=1, concat_axis=2, tiled=True)  82.9 us
    all_to_all x2, blocking collectives, transpose_apply(): lax.all_to_all(images, 'lag', split_axis=2, concat_axis=1, tiled=True)  72.3 us
    psum x2, blocking collectives, orthonormalize(): gram_matrix = lax.psum(partial_gram, 'lag') / lag_total  72 us
    all_gather x1, blocking collectives, on_device(): whole_corr = lax.all_gather(halved, 'lag', axis=1, tiled=True)  30.7 us
    div x2, local copies, waits for them, and re-layouts, local_inverse(): rotate(rotation(half_ids, first_ids, first, 1.0), sectioned, 'tk,aks->ats')  30.3 us
    all_to_all x5, local copies, waits for them, and re-layouts, transpose_apply(): lax.all_to_all(images, 'lag', split_axis=2, concat_axis=1, tiled=True)  29.9 us
  transfers between devices with their start and end apart: 4, of which 4 were waited for; matrix products, arithmetic and copies ran while one was open for 3% of the time, Pallas kernels for 0%

commit v1 on v0

--- a/solution.py
+++ b/solution.py
@@ -99,7 +99,10 @@
     spread = lax.all_to_all(columns, "lag", split_axis=1, concat_axis=2, tiled=True)
     length = spread.shape[2]
     images = local_inverse(local_forward(spread) * spec_table[None, None], length)
-    back = lax.all_to_all(images, "lag", split_axis=2, concat_axis=1, tiled=True)
+    size = lax.axis_size("lag")
+    shards = jnp.stack(jnp.split(images, size, axis=2), axis=0)
+    shards = lax.all_to_all(shards, "lag", split_axis=0, concat_axis=0)
+    back = jnp.concatenate(shards, axis=1)
     return back
 
 

time: 871 us -> 664 us (0.76)
  local copies, waits for them, and re-layouts: 221 us -> 39.2 us
  matrix products: 135 us -> 123 us
  other arithmetic: 53.5 us -> 42.4 us
    unnamed x44 -> x56, local copies, waits for them, and re-layouts: 132 us -> 11.7 us
    div x2 -> x0, local copies, waits for them, and re-layouts: 30.3 us -> none  [local_inverse(): rotate(rotation(half_ids, first_ids, first, 1.0), sectioned, 'tk,aks->ats')]
    all_to_all x5 -> x0, local copies, waits for them, and re-layouts: 29.9 us -> none  [transpose_apply(): lax.all_to_all(images, 'lag', split_axis=2, concat_axis=1, tiled=True)]
    dot_general x8, matrix products: 20.5 us -> 9.06 us  [accumulate(): jnp.einsum('ph,pcl->chl', high_hot, weighted, precision=exact)]
    all_to_all x2 -> x0, other arithmetic: 8.71 us -> none  [transpose_apply(): lax.all_to_all(images, 'lag', split_axis=2, concat_axis=1, tiled=True)]
  transfers between devices with their start and end apart: 4 -> 4, of which waited for: 4 -> 4; matrix products, arithmetic and copies ran while one was open for 3% -> 4% of each run, Pallas kernels for 0% -> 0%
where the time goes in v1:
time: 664 us; the launch traced here: 654 us
  waiting for transfers between devices  238 us (36%)
  blocking collectives  185 us (28%)
  matrix products  123 us (19%)
  other arithmetic  42.4 us (6%)
  local copies, waits for them, and re-layouts  39.2 us (6%)
  between operations  15.9 us (2%)
  starting transfers between devices  10.2 us (2%)
    unnamed x3, waiting for transfers between devices  137 us
    all_to_all x2, waiting for transfers between devices, transpose_apply(): lax.all_to_all(columns, 'lag', split_axis=1, concat_axis=2, tiled=True)  82.6 us
    all_to_all x2, blocking collectives, transpose_apply(): shards = lax.all_to_all(shards, 'lag', split_axis=0, concat_axis=0)  72.3 us
    psum x2, blocking collectives, orthonormalize(): gram_matrix = lax.psum(partial_gram, 'lag') / lag_total  71.5 us
    all_gather x1, blocking collectives, on_device(): whole_corr = lax.all_gather(halved, 'lag', axis=1, tiled=True)  30.7 us
    dot_general x10, matrix products, rotate(): jnp.einsum(form, sine, values[1], precision=exact)  24.5 us
    dot_general x9, matrix products, rotate(): jnp.einsum(form, cosine, values[1], precision=exact)  24.4 us
    dot_general x10, matrix products, rotate(): jnp.einsum(form, cosine, values[0], precision=exact)  23.8 us
  transfers between devices with their start and end apart: 4, of which 4 were waited for; matrix products, arithmetic and copies ran while one was open for 4% of the time, Pallas kernels for 0%

profile of v1, /device:TPU:2, one launch (start us, length us, event | category | flops | bytes accessed | tf_op | source)
XLA Modules:
  0.0 653.6 jit_solution(14652727903545321896)
XLA Ops:
  12.3 6.0 all-to-all-start
  19.7 54.4 %all-to-all-done = f32[2,96,2048]{2,0,1:T(2,128)S(1)} async-done(((f32[2,96,2048]{2,0,1:T(2,128)}), f32[2,96,2048]{2,0,1:T(2,128)S(1)}, u32[]{:S(2)}, u32[]{:S(2)}) %all-to-all-start) | async-done | bytes 1572896 | tf_op jit(solution)/shard_map/all_to_all | solution.py:99
  90.2 17.7 %all-gather.2.cloned.1.call-done = bf16[2,4096,256]{1,2,0:T(8,128)(2,1)} async-done(((bf16[2,4096,32]{1,2,0:T(8,128)(2,1)}), bf16[2,4096,256]{1,2,0:T(8,128)(2,1)}) %all-gather.2.cloned.1.call-update) | async-done | bytes 4194320 | tf_op jit(solution)/shard_map/all_gather | solution.py:125
  114.4 13.3 %while.17 = (s32[]{:T(128)}, f32[3,128,128]{1,2,0:T(8,128)S(1)}, f32[8192,3]{0,1:T(4,128)S(1)}, s32[8192]{0:T(1024)S(1)}, s32[]{:T(128)}, /*index=5*/s32[]{:T(128)}, s32[]{:T(128)}, s32[]{:T(128)}) while((s32[]{:T(128)}, f32[3,128,128]{1,2,0:T(8,128)S(1)}, f32[8192,3]{0,1:T(4,128)S(1)}, s32[8192]{0:T(1024)S(1)}, ...), condition=%wide.region_1.2_spmd.clone.clone, body=%wide.region_0.1_spmd.clone.clone.sunk | while | flops 605024256 | bytes 2560157 | solution.py:41
  128.0 5.1 copy.139
  134.5 4.4 subtract_bitcast_fusion.1
  141.8 137.5 %reduce-scatter.4.cloned.1.call-done = f32[2048,3]{1,0:T(8,128)} async-done(((f32[16384,3]{1,0:T(8,128)}), f32[2048,3]{1,0:T(8,128)}) %reduce-scatter.4.cloned.1.call-update) | async-done | bytes 24592
  280.8 10.4 %all-reduce = (f32[2,2048]{1,0:T(2,128)S(1)}, f32[]{:T(128)}) all-reduce(f32[2,2048]{1,0:T(2,128)S(1)} %slice.94, f32[]{:T(128)S(6)} %convert_element_type.188), channel_id=1, replica_groups=mesh['snap'=4,'lag'=8] {'snap'}, use_global_device_ids=true, to_apply=%region_3.4 | all-reduce | flops 4097 | bytes 32776 | tf_op jit(solution)/shard_map/psum | solution.py:142
  292.5 30.7 %all_gather.7 = f32[2,16384]{1,0:T(2,128)S(1)} all-gather(f32[2,2048]{1,0:T(2,128)S(1)} %get-tuple-element.212), channel_id=1, replica_groups=mesh['snap'=4,'lag'=8] {'lag'}, dimensions={1}, use_global_device_ids=true | all-gather | bytes 147456 | tf_op jit(solution)/shard_map/all_gather | solution.py:149
  336.4 3.1 fusion.66
  339.5 4.0 fusion.65
  343.5 4.0 fusion.51
  352.0 5.3 fusion.50
  360.5 35.2 %all_to_all.40 = f32[8,2,12,2048]{3,1,2,0:T(2,128)S(1)} all-to-all(f32[8,2,12,2048]{3,1,2,0:T(2,128)S(1)} %copy.89), channel_id=1, replica_groups=mesh['snap'=4,'lag'=8] {'lag'}, dimensions={0} | all-to-all | bytes 3145728 | tf_op jit(solution)/shard_map/all_to_all | solution.py:104
  395.7 3.1 fusion.55
  398.8 35.6 %psum.30 = f32[96,96]{0,1:T(8,128)S(1)} all-reduce(f32[96,96]{0,1:T(8,128)S(1)} %fusion.55), channel_id=1, replica_groups=mesh['snap'=4,'lag'=8] {'lag'}, use_global_device_ids=true, to_apply=%region_5.6 | all-reduce | flops 9216 | bytes 73728 | tf_op jit(solution)/shard_map/psum | solution.py:111
  434.5 8.8 %cholesky.44 = f32[96,96]{1,0:T(8,128)S(1)} custom-call(f32[96,96]{1,0:T(8,128)S(1)} %fusion.202), custom_call_target="Cholesky" | custom-call | tf_op jit(solution)/shard_map/jit(cholesky)/cholesky | solution.py:112
  444.6 7.4 %custom-call.7 = f32[1,96,96]{1,2,0:T(8,128)S(1)} custom-call(f32[1,96,96]{2,1,0:T(8,128)S(1)} %fusion.197), custom_call_target="InvertDiagBlocksLowerTriangular" | custom-call | tf_op jit(solution)/shard_map/triangular_solve/custom-call.0 | solution.py:113
  457.0 4.1 all-to-all-start.2
  461.4 28.3 %all-to-all-done.2 = f32[2,96,2048]{2,0,1:T(2,128)S(1)} async-done(((f32[2,96,2048]{2,0,1:T(2,128)}), f32[2,96,2048]{2,0,1:T(2,128)S(1)}, u32[]{:S(2)}, u32[]{:S(2)}) %all-to-all-start.2) | async-done | bytes 1572896 | tf_op jit(solution)/shard_map/all_to_all | solution.py:99
  500.1 3.3 convolution_subtract_fusion.1
  505.4 3.1 fusion.73
  524.5 3.1 fusion.68
  527.6 4.0 fusion.67
  531.6 4.4 fusion.49
  540.5 5.1 fusion.48
  548.9 37.2 %all_to_all.41 = f32[8,2,12,2048]{3,1,2,0:T(2,128)S(1)} all-to-all(f32[8,2,12,2048]{3,1,2,0:T(2,128)S(1)} %copy.113), channel_id=1, replica_groups=mesh['snap'=4,'lag'=8] {'lag'}, dimensions={0} | all-to-all | bytes 3145728 | tf_op jit(solution)/shard_map/all_to_all | solution.py:104
  586.0 3.1 fusion.58
  589.1 36.0 %psum.31 = f32[96,96]{0,1:T(8,128)S(1)} all-reduce(f32[96,96]{0,1:T(8,128)S(1)} %fusion.58), channel_id=1, replica_groups=mesh['snap'=4,'lag'=8] {'lag'}, use_global_device_ids=true, to_apply=%region_8.11 | all-reduce | flops 9216 | bytes 73728 | tf_op jit(solution)/shard_map/psum | solution.py:111
  625.2 8.8 %cholesky.55 = f32[96,96]{1,0:T(8,128)S(1)} custom-call(f32[96,96]{1,0:T(8,128)S(1)} %fusion.200), custom_call_target="Cholesky" | custom-call | tf_op jit(solution)/shard_map/jit(cholesky)/cholesky | solution.py:112
  635.3 7.4 %custom-call.8 = f32[1,96,96]{1,2,0:T(8,128)S(1)} custom-call(f32[1,96,96]{2,1,0:T(8,128)S(1)} %fusion.198), custom_call_target="InvertDiagBlocksLowerTriangular" | custom-call | tf_op jit(solution)/shard_map/triangular_solve/custom-call.0 | solution.py:113
  643.0 3.6 convolution_bitcast_fusion
  (205 shorter events, 113.6 us)
Async XLA Ops:
  7.2 2.7 copy-start.12
  7.2 100.7 %all-gather.2.cloned.1.call-start = ((), (), s32[]{:S(2)}) async-start(), calls=%async_computation.5 | async-start | bytes 4718592 | tf_op jit(solution)/shard_map/all_gather | solution.py:125
  12.3 6.0 copy-start.15
  12.3 61.8 %all-to-all-start = ((f32[2,96,2048]{2,0,1:T(2,128)}), f32[2,96,2048]{2,0,1:T(2,128)S(1)}, u32[]{:S(2)}, u32[]{:S(2)}) async-start(f32[2,96,2048]{2,0,1:T(2,128)} %copy.80), calls=%async_computation | async-start | bytes 3145728 | tf_op jit(solution)/shard_map/all_to_all | solution.py:99
  18.2 261.0 %reduce-scatter.4.cloned.1.call-start = ((), (), s32[]{:S(2)}) async-start(), calls=%async_computation.6 | async-start | bytes 9437184
  19.2 67.8 %copy-start.5 = (f32[256,128]{1,0:T(8,128)}, f32[256,128]{1,0:T(8,128)S(1)}, u32[]{:S(2)}) copy-start(f32[256,128]{1,0:T(8,128)S(1)} %get-tuple-element.220) | copy-start | bytes 393220
  84.0 2.9 copy-start
  86.9 21.0 %copy-start.11 = (bf16[2,4096,32]{1,2,0:T(8,128)(2,1)S(1)}, bf16[2,4096,32]{1,2,0:T(8,128)(2,1)}, u32[]{:S(2)}) copy-start(bf16[2,4096,32]{1,2,0:T(8,128)(2,1)} %broadcast_select_fusion) | copy-start | bytes 1572868
  107.9 4.9 copy-start.16
  133.1 1.4 copy-start.1
  134.5 4.4 copy-start.2
  134.5 4.4 copy-start.6
  324.1 4.5 copy-start.4
  324.9 3.7 copy-start.3
  328.6 0.6 copy-start.13
  357.3 1.7 copy-start.9
  457.0 4.1 copy-start.7
  457.0 32.6 %all-to-all-start.2 = ((f32[2,96,2048]{2,0,1:T(2,128)}), f32[2,96,2048]{2,0,1:T(2,128)S(1)}, u32[]{:S(2)}, u32[]{:S(2)}) async-start(f32[2,96,2048]{2,0,1:T(2,128)} %copy.95), calls=%async_computation.2 | async-start | bytes 3145728 | tf_op jit(solution)/shard_map/all_to_all | solution.py:99
  495.6 1.9 copy-start.10
  514.3 2.9 copy-start.14
  545.6 1.7 copy-start.8
Sparse Core Ops, SparseCore 0:
  10.2 97.6 all-gather.1
  133.2 145.9 reduce-scatter.3
